TPU v7x, 32 devices: a whole 2x2x4 slice. The times are simulated.
32 devices in a mesh: expert: 16 (over z, y, core), tensor: 2 (over x).
Axes of the slice: x: 2, y: 2, z: 4, core: 2. Of those that a mesh axis runs over, the one named last changes fastest.
Arguments:
- tokens: bfloat16 [64, 256, 1280], P(('expert', 'tensor')), may hold values from -6 to 6
- slot_keys: bfloat16 [1280, 16], replicated, may hold values from -6 to 6
- logit_scale: float32 [], replicated, may hold values from 40 to 80
- w_in: bfloat16 [16, 1280, 3584], P('expert', None, 'tensor'), may hold values from -0.625 to 0.625
- b_in: bfloat16 [16, 3584], P('expert', 'tensor'), may hold values from -3 to 3
- w_out: bfloat16 [16, 3584, 1280], P('expert', 'tensor'), may hold values from -0.09375 to 0.09375
- b_out: bfloat16 [16, 1280], P('expert'), may hold values from -3 to 3
Outputs:
- mixed: bfloat16 [64, 256, 1280], P(('expert', 'tensor'))
All inputs are finite; a program needn't handle non-finite values.
Results may differ from a plain program's by a relative error of at most 0.0071.
Values may be sent and summed in bfloat16 or wider, within the bound.
A program may use at most 64 MiB of HBM per device.

v0:
```python
import jax
import jax.numpy as jnp
from jax import lax
from jax.sharding import PartitionSpec as P

EPS = 1e-06


def local(tokens, slot_keys, logit_scale, w_in, b_in, w_out, b_out):
    images, seq_len, width = tokens.shape
    slots = slot_keys.shape[1]
    row_sq = jnp.sum(jnp.square(tokens.astype(jnp.float32)), axis=2, keepdims=True)
    row_inv = lax.rsqrt(row_sq + EPS)
    key_sq = jnp.sum(jnp.square(slot_keys.astype(jnp.float32)), axis=0)
    key_inv = lax.rsqrt(key_sq + EPS)
    raw = jnp.dot(
        tokens.reshape(images * seq_len, width), slot_keys, preferred_element_type=jnp.float32
    )
    logits = logit_scale * row_inv * key_inv * raw.reshape(images, seq_len, slots)
    expo = jnp.exp(logits)
    dispatch = (expo / jnp.sum(expo, axis=1, keepdims=True)).astype(jnp.bfloat16)
    combine = (expo / jnp.sum(expo, axis=2, keepdims=True)).astype(jnp.bfloat16)
    slot_in = jnp.einsum(
        "ims,imd->isd", dispatch, tokens, preferred_element_type=jnp.float32
    ).astype(jnp.bfloat16)
    routed = lax.all_to_all(slot_in, "expert", split_axis=1, concat_axis=0, tiled=True)
    bias_wide = b_in.astype(jnp.float32)
    pre = (
        jnp.einsum(
            "rkd,kdf->rkf",
            lax.all_gather(routed, "tensor", axis=0, tiled=True),
            w_in,
            preferred_element_type=jnp.float32,
        )
        + bias_wide[None]
    )
    hidden = jax.nn.gelu(pre).astype(jnp.bfloat16)
    mine = lax.psum_scatter(
        jnp.einsum("rkf,kfd->rkd", hidden, w_out, preferred_element_type=jnp.float32),
        "tensor",
        scatter_dimension=0,
        tiled=True,
    )
    slot_out = (mine + b_out.astype(jnp.float32)[None]).astype(jnp.bfloat16)
    returned = lax.all_to_all(slot_out, "expert", split_axis=0, concat_axis=1, tiled=True)
    mixed = jnp.einsum("ims,isd->imd", combine, returned, preferred_element_type=jnp.float32)
    return mixed.astype(jnp.bfloat16)


def solution(mesh):
    placed = (
        P(("expert", "tensor"), None, None),
        P(),
        P(),
        P("expert", None, "tensor"),
        P("expert", "tensor"),
        P("expert", "tensor", None),
        P("expert", None),
    )
    return jax.shard_map(
        local,
        mesh=mesh,
        in_specs=placed,
        out_specs=P(("expert", "tensor"), None, None),
        check_vma=False,
    )
```

profile of v0, /device:TPU:0, one launch (start us, length us, event | category | flops | bytes accessed | tf_op | source)
XLA Modules:
  0.0 72.5 jit_solution(5864950734486424679)
XLA Ops:
  6.5 0.0 copy-start
  6.5 0.0 copy-start.1
  7.3 0.9 %multiply_reduce_fusion.1 = f32[16]{0:T(128)S(1)} fusion(bf16[1280,16]{0,1:T(8,128)(2,1)} %param.8), kind=kLoop, calls=%fused_computation.32 | loop fusion | flops 61424 | bytes 41024 | tf_op jit(solution)/shard_map/reduce_sum | solution.py:14
  8.2 1.7 %multiply_reduce_fusion = f32[2,256]{1,0:T(2,128)S(1)} fusion(bf16[2,256,1280]{2,1,0:T(8,128)(2,1)} %param.7), kind=kLoop, calls=%fused_computation.5 | loop fusion | flops 1965568 | bytes 1312768 | tf_op jit(solution)/shard_map/reduce_sum | solution.py:12
  9.9 1.8 %fusion.16 = f32[2,256,16]{1,2,0:T(8,128)S(1)} fusion(bf16[2,256,1280]{2,1,0:T(8,128)(2,1)} %param.7, bf16[1280,16]{0,1:T(8,128)(2,1)} %param.8, f32[16]{0:T(128)S(1)} %add_rsqrt_fusion, f32[2,256]{1,0:T(2,128)S(1)} %rsqrt_multiply_fusion), kind=kOutput, calls=%fused_computation.12 | convolution fusion | flops 20987904 | bytes 1386560 | tf_op jit(solution)/shard_map/dot_general | solution.py:16
  11.7 0.0 copy-done
  11.7 0.3 convolution_convert_fusion.1
  12.0 0.7 copy.13
  12.7 7.4 %all-to-all-start = ((bf16[2,16,1280]{2,0,1:T(2,128)(2,1)}), bf16[2,16,1280]{2,0,1:T(2,128)(2,1)S(1)}, u32[]{:S(2)}, u32[]{:S(2)}) async-start(bf16[2,16,1280]{2,0,1:T(2,128)(2,1)} %copy.13), calls=%async_computation | async-start | bytes 163840 | tf_op jit(solution)/shard_map/all_to_all | solution.py:26
  20.1 0.0 reduce-scatter.2.cloned.1.call-start
  20.2 0.0 copy-done.1
  20.2 7.0 %all-to-all-done = bf16[2,16,1280]{2,0,1:T(2,128)(2,1)S(1)} async-done(((bf16[2,16,1280]{2,0,1:T(2,128)(2,1)}), bf16[2,16,1280]{2,0,1:T(2,128)(2,1)S(1)}, u32[]{:S(2)}, u32[]{:S(2)}) %all-to-all-start) | async-done | bytes 81952 | tf_op jit(solution)/shard_map/all_to_all | solution.py:26
  27.3 5.1 %all_gather.3 = bf16[64,1,1280]{2,0,1:T(8,128)(2,1)S(1)} all-gather(bf16[32,1,1280]{2,0,1:T(8,128)(2,1)S(1)} %all_to_all.29), channel_id=1, replica_groups=mesh['expert'=16,'tensor'=2] {'tensor'}, dimensions={0}, use_global_device_ids=true | all-gather | bytes 245760 | tf_op jit(solution)/shard_map/all_gather | solution.py:31
  32.4 0.0 copy-start.2
  32.4 6.3 %fusion.4 = f32[64,1,1280]{2,0,1:T(8,128)} fusion(bf16[1,1792,1280]{2,1,0:T(8,128)(2,1)} %param.12, bf16[1,1280,1792]{2,1,0:T(8,128)(2,1)} %param.10, f32[1792]{0:T(1024)S(1)} %convert_reduce_fusion, bf16[64,1,1280]{2,0,1:T(8,128)(2,1)S(1)} %all_gather.3), kind=kOutput, calls=%fused_computation.6 | convolution fusion | flops 588349440 | bytes 9673728 | tf_op jit(solution)/shard_map/rkf,kfd->rkd/dot_general | solution.py:39
  38.7 0.0 reduce-scatter.2.cloned.1.call-update
  38.7 0.0 copy-done.2
  38.7 10.0 %reduce-scatter.2.cloned.1.call-done = f32[32,1,1280]{2,0,1:T(8,128)} async-done(((f32[64,1,1280]{2,0,1:T(8,128)}), f32[32,1,1280]{2,0,1:T(8,128)}) %reduce-scatter.2.cloned.1.call-update) | async-done | bytes 163856 | tf_op jit(solution)/shard_map/reduce_scatter | solution.py:38
  48.7 0.9 %add_convert_fusion = bf16[32,1,1280]{2,0,1:T(8,128)(2,1)S(1)} fusion(f32[32,1,1280]{2,0,1:T(8,128)} %reduce-scatter.2.cloned.1.call-done, f32[1280]{0:T(1024)S(1)} %convert_reduce_fusion.1), kind=kLoop, calls=%fused_computation.29 | loop fusion | flops 81920 | bytes 250880 | tf_op jit(solution)/shard_map/convert_element_type | solution.py:44
  49.7 0.5 broadcast.27
  50.2 0.7 reduce.5
  50.9 12.5 %all_to_all.36 = bf16[16,2,1280]{2,1,0:T(2,128)(2,1)S(1)} all-to-all(bf16[16,2,1280]{2,1,0:T(2,128)(2,1)S(1)} %reshape.50), channel_id=1, replica_groups=mesh['expert'=16,'tensor'=2] {'expert'}, dimensions={0} | all-to-all | bytes 163840 | tf_op jit(solution)/shard_map/all_to_all | solution.py:45
  63.4 0.1 reshape.51
  63.5 0.5 reduce.2
  64.0 1.6 %convolution_convert_fusion = bf16[2,256,1280]{2,1,0:T(8,128)(2,1)} fusion(bf16[16,2,1,1280]{3,1,0,2:T(2,128)(2,1)S(1)} %all_to_all.31, f32[2,256,16]{1,2,0:T(8,128)S(1)} %fusion.16), kind=kOutput, calls=%fused_computation.4 | convolution fusion | flops 21643792 | bytes 1425408 | tf_op jit(solution)/shard_map/ims,isd->imd/dot_general | solution.py:46
  (7 shorter events, 0.2 us)
Async XLA Ops:
  6.5 5.1 %copy-start = (bf16[2,256,1280]{2,1,0:T(8,128)(2,1)S(1)}, bf16[2,256,1280]{2,1,0:T(8,128)(2,1)}, u32[]{:S(2)}) copy-start(bf16[2,256,1280]{2,1,0:T(8,128)(2,1)} %param.7) | copy-start | bytes 3932164
  6.5 13.6 %copy-start.1 = (bf16[1,1792]{1,0:T(2,128)(2,1)S(1)}, bf16[1,1792]{1,0:T(2,128)(2,1)}, u32[]{:S(2)}) copy-start(bf16[1,1792]{1,0:T(2,128)(2,1)} %param.11) | copy-start | bytes 10756
  12.7 14.5 %all-to-all-start = ((bf16[2,16,1280]{2,0,1:T(2,128)(2,1)}), bf16[2,16,1280]{2,0,1:T(2,128)(2,1)S(1)}, u32[]{:S(2)}, u32[]{:S(2)}) async-start(bf16[2,16,1280]{2,0,1:T(2,128)(2,1)} %copy.13), calls=%async_computation | async-start | bytes 163840 | tf_op jit(solution)/shard_map/all_to_all | solution.py:26
  20.1 28.6 %reduce-scatter.2.cloned.1.call-start = ((), (), s32[]{:S(2)}) async-start(), calls=%async_computation.3 | async-start | bytes 491520 | tf_op jit(solution)/shard_map/reduce_scatter | solution.py:38
  32.4 6.3 %copy-start.2 = (bf16[1,1280]{1,0:T(2,128)(2,1)S(1)}, bf16[1,1280]{1,0:T(2,128)(2,1)}, u32[]{:S(2)}) copy-start(bf16[1,1280]{1,0:T(2,128)(2,1)} %param.13) | copy-start | bytes 7684
Sparse Core Ops, SparseCore 0:
  38.8 9.8 reduce-scatter.1
where the time goes:
time: 72.8 us; the launch traced here: 72.5 us
  blocking collectives  17.6 us (24%)
  waiting for transfers between devices  17.1 us (23%)
  between operations  14.3 us (20%)
  matrix products  9.99 us (14%)
  starting transfers between devices  7.46 us (10%)
  other arithmetic  4.67 us (6%)
  local copies, waits for them, and re-layouts  1.4 us (2%)
    all_to_all x1, blocking collectives, local(): lax.all_to_all(slot_out, 'expert', split_axis=0, concat_axis=1, tiled=True)  12.5 us
    reduce_scatter x1, waiting for transfers between devices, local(): lax.psum_scatter(jnp.einsum('rkf,kfd->rkd', hidden, w_out, preferred_elem...  10 us
    all_to_all x1, starting transfers between devices, local(): lax.all_to_all(slot_in, 'expert', split_axis=1, concat_axis=0, tiled=True)  7.41 us
    all_to_all x1, waiting for transfers between devices, local(): lax.all_to_all(slot_in, 'expert', split_axis=1, concat_axis=0, tiled=True)  7.02 us
    dot_general x1, matrix products, local(): jnp.einsum('rkf,kfd->rkd', hidden, w_out, preferred_element_type=jnp.floa...  6.26 us
    all_gather x1, blocking collectives, local(): lax.all_gather(routed, 'tensor', axis=0, tiled=True)  5.11 us
    dot_general x1, matrix products, local(): jnp.dot(tokens.reshape(images * seq_len, width), slot_keys, preferred_ele...  1.78 us
    reduce_sum x1, other arithmetic, local(): jnp.sum(jnp.square(tokens.astype(jnp.float32)), axis=2, keepdims=True)  1.65 us
  transfers between devices with their start and end apart: 2, of which 2 were waited for; matrix products, arithmetic and copies ran while one was open for 0% of the time, Pallas kernels for 0%

commit v1 on v0

--- a/solution.py
+++ b/solution.py
@@ -4,6 +4,21 @@
 from jax.sharding import PartitionSpec as P
 
 EPS = 1e-06
+
+
+def on_each_block(value, axis, dim, make, out_dim):
+    ways, here, step = (lax.axis_size(axis), lax.axis_index(axis), value.shape[dim])
+    results = []
+    for far in range(ways):
+        arriving = (
+            lax.ppermute(value, axis, [(d, (d + 1) % ways) for d in range(ways)])
+            if far + 1 < ways
+            else value
+        )
+        results.append(make(value, (here - far) % ways * step))
+        value = arriving
+    line = jnp.concatenate(results[::-1], axis=out_dim)
+    return jnp.roll(line, (here + 1) * results[0].shape[out_dim], axis=out_dim)
 
 
 def local(tokens, slot_keys, logit_scale, w_in, b_in, w_out, b_out):
@@ -26,11 +41,14 @@
     routed = lax.all_to_all(slot_in, "expert", split_axis=1, concat_axis=0, tiled=True)
     bias_wide = b_in.astype(jnp.float32)
     pre = (
-        jnp.einsum(
-            "rkd,kdf->rkf",
-            lax.all_gather(routed, "tensor", axis=0, tiled=True),
-            w_in,
-            preferred_element_type=jnp.float32,
+        on_each_block(
+            routed,
+            "tensor",
+            0,
+            lambda part, start: jnp.einsum(
+                "rkd,kdf->rkf", part, w_in, preferred_element_type=jnp.float32
+            ),
+            0,
         )
         + bias_wide[None]
     )

time: 72.8 us -> 69.7 us (0.957)
  blocking collectives: 17.6 us -> 12.5 us
  starting transfers between devices: 7.46 us -> 9.01 us
  local copies, waits for them, and re-layouts: 1.4 us -> 2.82 us
    all_gather x1 -> x0, blocking collectives: 5.11 us -> none  [local(): lax.all_gather(routed, 'tensor', axis=0, tiled=True)]
    dot_general x1, matrix products: 6.26 us -> 1.76 us  [local(): jnp.einsum('rkf,kfd->rkd', hidden, w_out, preferred_element_type=jnp.floa...]
    dot_general x0 -> x2, matrix products: none -> 4.11 us  [local(): jnp.einsum('rkd,kdf->rkf', part, w_in, preferred_element_type=jnp.float32)]
    ppermute x0 -> x1, starting transfers between devices: none -> 1.56 us  [on_each_block(): lax.ppermute(value, axis, [(d, (d + 1) % ways) for d in range(ways)])]
    unnamed x8 -> x12, local copies, waits for them, and re-layouts: 0.11 us -> 1.49 us
  transfers between devices with their start and end apart: 2 -> 3, of which waited for: 2 -> 2; matrix products, arithmetic and copies ran while one was open for 0% -> 5% of each run, Pallas kernels for 0% -> 0%
where the time goes in v1:
time: 69.7 us; the launch traced here: 69.3 us
  waiting for transfers between devices  16.4 us (24%)
  between operations  14.3 us (21%)
  blocking collectives  12.5 us (18%)
  matrix products  9.59 us (14%)
  starting transfers between devices  9.01 us (13%)
  other arithmetic  4.67 us (7%)
  local copies, waits for them, and re-layouts  2.82 us (4%)
    all_to_all x1, blocking collectives, local(): lax.all_to_all(slot_out, 'expert', split_axis=0, concat_axis=1, tiled=True)  12.5 us
    reduce_scatter x1, waiting for transfers between devices, local(): lax.psum_scatter(jnp.einsum('rkf,kfd->rkd', hidden, w_out, preferred_elem...  9.35 us
    all_to_all x1, starting transfers between devices, local(): lax.all_to_all(slot_in, 'expert', split_axis=1, concat_axis=0, tiled=True)  7.41 us
    all_to_all x1, waiting for transfers between devices, local(): lax.all_to_all(slot_in, 'expert', split_axis=1, concat_axis=0, tiled=True)  7 us
    dot_general x2, matrix products, local(): jnp.einsum('rkd,kdf->rkf', part, w_in, preferred_element_type=jnp.float32)  4.11 us
    dot_general x1, matrix products, local(): jnp.dot(tokens.reshape(images * seq_len, width), slot_keys, preferred_ele...  1.78 us
    dot_general x1, matrix products, local(): jnp.einsum('rkf,kfd->rkd', hidden, w_out, preferred_element_type=jnp.floa...  1.76 us
    reduce_sum x1, other arithmetic, local(): jnp.sum(jnp.square(tokens.astype(jnp.float32)), axis=2, keepdims=True)  1.65 us
  transfers between devices with their start and end apart: 3, of which 2 were waited for; matrix products, arithmetic and copies ran while one was open for 5% of the time, Pallas kernels for 0%

profile of v1, /device:TPU:0, one launch (start us, length us, event | category | flops | bytes accessed | tf_op | source)
XLA Modules:
  0.0 69.3 jit_solution(7838184708127693751)
XLA Ops:
  6.5 0.0 copy-start.1
  6.5 0.0 copy-start.2
  7.3 0.9 %multiply_reduce_fusion.1 = f32[16]{0:T(128)S(1)} fusion(bf16[1280,16]{0,1:T(8,128)(2,1)} %param.8), kind=kLoop, calls=%fused_computation.40 | loop fusion | flops 61424 | bytes 41024 | tf_op jit(solution)/shard_map/reduce_sum | solution.py:29
  8.2 1.7 %multiply_reduce_fusion = f32[2,256]{1,0:T(2,128)S(1)} fusion(bf16[2,256,1280]{2,1,0:T(8,128)(2,1)} %param.7), kind=kLoop, calls=%fused_computation.7 | loop fusion | flops 1965568 | bytes 1312768 | tf_op jit(solution)/shard_map/reduce_sum | solution.py:27
  9.9 1.8 %fusion.15 = f32[2,256,16]{1,2,0:T(8,128)S(1)} fusion(bf16[2,256,1280]{2,1,0:T(8,128)(2,1)} %param.7, bf16[1280,16]{0,1:T(8,128)(2,1)} %param.8, f32[16]{0:T(128)S(1)} %add_rsqrt_fusion, f32[2,256]{1,0:T(2,128)S(1)} %rsqrt_multiply_fusion), kind=kOutput, calls=%fused_computation.13 | convolution fusion | flops 20987904 | bytes 1386560 | tf_op jit(solution)/shard_map/dot_general | solution.py:31
  11.7 0.0 copy-done.1
  11.7 0.3 convolution_convert_fusion.1
  12.0 0.7 %copy.14 = bf16[2,16,1280]{2,0,1:T(2,128)(2,1)} copy(bf16[2,16,1280]{2,1,0:T(8,128)(2,1)S(1)} %convolution_convert_fusion.1) | data formatting | bytes 163840 | tf_op jit(solution)/shard_map/convert_element_type | solution.py:40
  12.7 7.4 %all-to-all-start = ((bf16[2,16,1280]{2,0,1:T(2,128)(2,1)}), bf16[2,16,1280]{2,0,1:T(2,128)(2,1)S(1)}, u32[]{:S(2)}, u32[]{:S(2)}) async-start(bf16[2,16,1280]{2,0,1:T(2,128)(2,1)} %copy.14), calls=%async_computation | async-start | bytes 163840 | tf_op jit(solution)/shard_map/all_to_all | solution.py:41
  20.1 0.0 reduce-scatter.2.cloned.1.call-start
  20.2 0.0 copy-done.2
  20.2 7.0 %all-to-all-done = bf16[2,16,1280]{2,0,1:T(2,128)(2,1)S(1)} async-done(((bf16[2,16,1280]{2,0,1:T(2,128)(2,1)}), bf16[2,16,1280]{2,0,1:T(2,128)(2,1)S(1)}, u32[]{:S(2)}, u32[]{:S(2)}) %all-to-all-start) | async-done | bytes 81952 | tf_op jit(solution)/shard_map/all_to_all | solution.py:41
  27.3 0.0 copy-start
  27.3 1.6 %collective-permute-start = (bf16[32,1,1280]{2,0,1:T(8,128)(2,1)S(1)}, bf16[32,1,1280]{2,0,1:T(8,128)(2,1)S(1)}, u32[]{:S(2)}, u32[]{:S(2)}) collective-permute-start(bf16[32,1,1280]{2,0,1:T(8,128)(2,1)S(1)} %all_to_all.29), channel_id=1, source_target_pairs={{0,1},{1,0},{2,3},{3,2},{4,5},{5,4},{6,7},{7,6},{8,9},{9,8},{10,11... | collective-permute-start | bytes 245768 | tf_op jit(solution)/shard_map/ppermute | solution.py:14
  28.9 3.2 %fusion.12 = f32[32,1,1792]{2,0,1:T(8,128)S(1)} fusion(bf16[32,1280]{1,0:T(8,128)(2,1)S(1)} %reshape.48, bf16[1,1280,1792]{2,1,0:T(8,128)(2,1)} %param.10), kind=kOutput, calls=%fused_computation.10 | convolution fusion | flops 146800640 | bytes 4898816 | tf_op jit(solution)/shard_map/rkd,kdf->rkf/dot_general | solution.py:48
  32.1 0.0 copy-start.4
  32.1 0.0 collective-permute-done
  32.1 0.0 copy-done
  32.1 0.9 %fusion.9 = f32[32,1,1792]{2,0,1:T(8,128)S(1)} fusion(bf16[1,1280,1792]{2,1,0:T(8,128)(2,1)S(1)} %copy-done, bf16[32,1,1280]{2,0,1:T(8,128)(2,1)S(1)} %collective-permute-done), kind=kOutput, calls=%fused_computation.9 | convolution fusion | flops 146800640 | bytes 4898816 | tf_op jit(solution)/shard_map/rkd,kdf->rkf/dot_general | solution.py:48
  33.0 1.4 %copy-done.4 = bf16[1,1792,1280]{2,1,0:T(8,128)(2,1)S(1)} copy-done((bf16[1,1792,1280]{2,1,0:T(8,128)(2,1)S(1)}, bf16[1,1792,1280]{2,1,0:T(8,128)(2,1)}, u32[]{:S(2)}) %copy-start.4) | copy-done | bytes 4587544
  34.4 0.0 copy-start.3
  34.4 1.8 %fusion.6 = f32[64,1,1280]{2,0,1:T(8,128)} fusion(bf16[1,1792,1280]{2,1,0:T(8,128)(2,1)S(1)} %copy-done.4, s32[]{:T(128)S(6)} %select_n.14, f32[32,1,1792]{2,0,1:T(8,128)S(1)} %fusion.9, f32[32,1,1792]{2,0,1:T(8,128)S(1)} %fusion.12, f32[1792]{0:T(1024)S(1)} %convert_reduce_fusion), kind=kOutput, calls=%fused_computation.8 | convolution fusion | flops 295092224 | bytes 5381124 | tf_op jit(solution)/shard_map/rkf,kfd->rkd/dot_general | solution.py:57
  36.2 0.0 reduce-scatter.2.cloned.1.call-update
  36.2 0.0 copy-done.3
  36.2 9.3 %reduce-scatter.2.cloned.1.call-done = f32[32,1,1280]{2,0,1:T(8,128)} async-done(((f32[64,1,1280]{2,0,1:T(8,128)}), f32[32,1,1280]{2,0,1:T(8,128)}) %reduce-scatter.2.cloned.1.call-update) | async-done | bytes 163856 | tf_op jit(solution)/shard_map/reduce_scatter | solution.py:56
  45.6 0.9 %add_convert_fusion = bf16[32,1,1280]{2,0,1:T(8,128)(2,1)S(1)} fusion(f32[32,1,1280]{2,0,1:T(8,128)} %reduce-scatter.2.cloned.1.call-done, f32[1280]{0:T(1024)S(1)} %convert_reduce_fusion.1), kind=kLoop, calls=%fused_computation.36 | loop fusion | flops 81920 | bytes 250880 | tf_op jit(solution)/shard_map/convert_element_type | solution.py:62
  46.5 0.5 broadcast.27
  47.0 0.7 reduce.5
  47.7 12.5 %all_to_all.36 = bf16[16,2,1280]{2,1,0:T(2,128)(2,1)S(1)} all-to-all(bf16[16,2,1280]{2,1,0:T(2,128)(2,1)S(1)} %reshape.57), channel_id=1, replica_groups=mesh['expert'=16,'tensor'=2] {'expert'}, dimensions={0} | all-to-all | bytes 163840 | tf_op jit(solution)/shard_map/all_to_all | solution.py:63
  60.3 0.1 reshape.58
  60.4 0.5 reduce.2
  60.9 1.6 %convolution_convert_fusion = bf16[2,256,1280]{2,1,0:T(8,128)(2,1)} fusion(bf16[16,2,1,1280]{3,1,0,2:T(2,128)(2,1)S(1)} %all_to_all.31, f32[2,256,16]{1,2,0:T(8,128)S(1)} %fusion.15), kind=kOutput, calls=%fused_computation.6 | convolution fusion | flops 21643792 | bytes 1425408 | tf_op jit(solution)/shard_map/ims,isd->imd/dot_general | solution.py:64
  (8 shorter events, 0.2 us)
Async XLA Ops:
  6.5 5.1 %copy-start.1 = (bf16[2,256,1280]{2,1,0:T(8,128)(2,1)S(1)}, bf16[2,256,1280]{2,1,0:T(8,128)(2,1)}, u32[]{:S(2)}) copy-start(bf16[2,256,1280]{2,1,0:T(8,128)(2,1)} %param.7) | copy-start | bytes 3932164
  6.5 13.7 %copy-start.2 = (bf16[1,1792]{1,0:T(2,128)(2,1)S(1)}, bf16[1,1792]{1,0:T(2,128)(2,1)}, u32[]{:S(2)}) copy-start(bf16[1,1792]{1,0:T(2,128)(2,1)} %param.11) | copy-start | bytes 10756
  12.7 14.5 %all-to-all-start = ((bf16[2,16,1280]{2,0,1:T(2,128)(2,1)}), bf16[2,16,1280]{2,0,1:T(2,128)(2,1)S(1)}, u32[]{:S(2)}, u32[]{:S(2)}) async-start(bf16[2,16,1280]{2,0,1:T(2,128)(2,1)} %copy.14), calls=%async_computation | async-start | bytes 163840 | tf_op jit(solution)/shard_map/all_to_all | solution.py:41
  20.1 25.4 %reduce-scatter.2.cloned.1.call-start = ((), (), s32[]{:S(2)}) async-start(), calls=%async_computation.3 | async-start | bytes 491520 | tf_op jit(solution)/shard_map/reduce_scatter | solution.py:56
  27.3 4.8 %copy-start = (bf16[1,1280,1792]{2,1,0:T(8,128)(2,1)S(1)}, bf16[1,1280,1792]{2,1,0:T(8,128)(2,1)}, u32[]{:S(2)}) copy-start(bf16[1,1280,1792]{2,1,0:T(8,128)(2,1)} %param.10) | copy-start | bytes 13762564
  27.3 4.8 %collective-permute-start = (bf16[32,1,1280]{2,0,1:T(8,128)(2,1)S(1)}, bf16[32,1,1280]{2,0,1:T(8,128)(2,1)S(1)}, u32[]{:S(2)}, u32[]{:S(2)}) collective-permute-start(bf16[32,1,1280]{2,0,1:T(8,128)(2,1)S(1)} %all_to_all.29), channel_id=1, source_target_pairs={{0,1},{1,0},{2,3},{3,2},{4,5},{5,4},{6,7},{7,6},{8,9},{9,8},{10,11... | collective-permute-start | bytes 245768 | tf_op jit(solution)/shard_map/ppermute | solution.py:14
  32.1 2.3 %copy-start.4 = (bf16[1,1792,1280]{2,1,0:T(8,128)(2,1)S(1)}, bf16[1,1792,1280]{2,1,0:T(8,128)(2,1)}, u32[]{:S(2)}) copy-start(bf16[1,1792,1280]{2,1,0:T(8,128)(2,1)} %param.12) | copy-start | bytes 13762564
  34.4 1.8 %copy-start.3 = (bf16[1,1280]{1,0:T(2,128)(2,1)S(1)}, bf16[1,1280]{1,0:T(2,128)(2,1)}, u32[]{:S(2)}) copy-start(bf16[1,1280]{1,0:T(2,128)(2,1)} %param.13) | copy-start | bytes 7684
Sparse Core Ops, SparseCore 0:
  36.3 9.2 reduce-scatter.1
